TPU v7x, 1024 devices: a whole 8x8x8 slice. The times are simulated.
1024 devices in a mesh: gx: 8 (over x_lo, core), gy: 16 (over x_hi, z), gz: 8 (over y).
Axes of the slice: x: 8 (x_hi: 2, x_lo: 4; x = x_hi * 4 + x_lo), y: 8, z: 8, core: 2. Of those that a mesh axis runs over, the one named last changes fastest.
Arguments:
- encoded: bfloat16 [8, 1024, 4096], P('gx', None, 'gy'), may hold values from -6 to 6
- lengths: int32 [8], P('gx'), may hold values from 128 to 1024, as said below
- kv_weight: bfloat16 [4096, 64, 128], P('gy', 'gz'), may hold values from -0.09375 to 0.09375
Outputs:
- keys_values: bfloat16 [8, 1024, 64, 128], P('gx', 'gy', 'gz')
Inputs may be any that keep to these rules, and one draw needn't show every extreme that they name: `lengths`: every length is a multiple of 128; some sequence has length 1024 and some has length 128.
All inputs are finite; a program needn't handle non-finite values.
Results may differ from a plain program's by a relative error of at most 0.001.
Values may be sent and summed in bfloat16 or wider, within the bound.
A program may use at most 32 MiB of HBM per device.

v0:
```python
import jax
import jax.numpy as jnp
from jax import lax
from jax.sharding import Mesh
from jax.sharding import PartitionSpec as P

GY = ("gy_0", "gy_1")


def sum_in_order(parts, axes, order):
    inside = parts.shape[1:]
    parts = parts.reshape(*(lax.axis_size(a) for a in axes), *inside)
    parts = jnp.moveaxis(parts, order, range(len(axes))).reshape(-1, *inside)
    for k in order:
        parts = lax.psum_scatter(parts, axes[k], scatter_dimension=0, tiled=True)
    return parts[0]


def split_up(shard, dim, peers):
    dims = shard.shape
    parts = shard.reshape(*dims[:dim], peers, dims[dim] // peers, *dims[dim + 1 :])
    return jnp.moveaxis(parts, dim, 0)


def scatter_axes(shard, axes, order, dim):
    peers = lax.axis_size(axes)
    return sum_in_order(split_up(shard, dim, peers), axes, order)


def local(encoded, lengths, kv_weight):
    seq_local, positions, width_local = encoded.shape
    depth_local = kv_weight.shape[1]
    pairs = kv_weight.shape[2]
    groups = lax.axis_size("gz")
    heads_local = pairs // 2 // groups
    rows_local = positions // lax.axis_size(GY)
    columns = depth_local * pairs
    weight = kv_weight.reshape(width_local, columns)
    partial_value = jnp.dot(
        encoded.reshape(seq_local * positions, width_local),
        weight,
        preferred_element_type=jnp.float32,
    )
    summed = scatter_axes(partial_value.reshape(seq_local, positions, columns), GY, (1, 0), 1)
    first_row = lax.axis_index(GY) * rows_local
    places = first_row + lax.broadcasted_iota(jnp.int32, (seq_local, rows_local), 1)
    keep = (places < lengths[:, None])[:, :, None]
    masked = jnp.where(keep, summed, jnp.zeros_like(summed)).astype(jnp.bfloat16)
    parts = masked.reshape(seq_local, rows_local, depth_local, 2, groups, heads_local)
    parts = jnp.transpose(parts, (4, 0, 1, 5, 3, 2)).reshape(
        groups, seq_local, rows_local, heads_local * 2 * depth_local
    )
    arrived = lax.all_to_all(parts, "gz", split_axis=0, concat_axis=0, tiled=True)
    arrived = arrived.reshape(groups, seq_local, rows_local, heads_local, 2, depth_local)
    arrived = jnp.transpose(arrived, (1, 2, 3, 4, 0, 5))
    return arrived.reshape(seq_local, rows_local, heads_local, 2 * depth_local * groups)


def solution(mesh):
    torus = Mesh(
        mesh.devices.reshape(mesh.shape["gx"], 2, 8, mesh.shape["gz"]), ("gx", "gy_0", "gy_1", "gz")
    )
    placed = (P("gx", None, GY), P("gx"), P(GY, "gz", None))
    return jax.shard_map(
        local, mesh=torus, in_specs=placed, out_specs=P("gx", GY, "gz", None), check_vma=False
    )
```

profile of v0, /device:TPU:2, one launch (start us, length us, event | category | flops | bytes accessed | tf_op | source)
XLA Modules:
  0.0 145.0 jit_solution(3735128303487960252)
XLA Ops:
  6.5 0.0 copy-start
  6.5 0.0 reduce-scatter.3.cloned.1.call-start
  6.5 1.3 reshape.68
  7.9 0.0 copy-done
  7.9 0.7 convolution_bitcast_fusion
  8.6 2.2 %copy.9 = f32[8,2,1,64,1024]{4,3,1,0,2:T(8,128)} copy(f32[8,2,1,64,1024]{4,3,0,1,2:T(8,128)S(1)} %convolution_bitcast_fusion) | data formatting | bytes 8388608 | tf_op jit(solution)/shard_map/transpose | solution.py:13
  10.8 0.0 reduce-scatter.3.cloned.1.call-update
  10.9 0.0 reduce-scatter.5.cloned.1.call-start
  10.9 74.1 %reduce-scatter.3.cloned.1.call-done = f32[2,1,64,1024]{3,2,0,1:T(8,128)} async-done(((f32[16,1,64,1024]{3,2,0,1:T(8,128)}), f32[2,1,64,1024]{3,2,0,1:T(8,128)}) %reduce-scatter.3.cloned.1.call-update) | async-done | bytes 524304 | tf_op jit(solution)/shard_map/reduce_scatter | solution.py:15
  85.0 0.0 reduce-scatter.5.cloned.1.call-update
  85.7 34.1 %reduce-scatter.5.cloned.1.call-done = f32[1,1,64,1024]{3,2,0,1:T(8,128)} async-done(((f32[2,1,64,1024]{3,2,0,1:T(8,128)}), f32[1,1,64,1024]{3,2,0,1:T(8,128)}) %reduce-scatter.5.cloned.1.call-update) | async-done | bytes 262160 | tf_op jit(solution)/shard_map/reduce_scatter | solution.py:15
  119.8 1.1 copy.10
  120.9 0.1 fusion.1
  121.0 0.2 copy.11
  121.1 0.1 copy.12
  121.3 15.9 %all_to_all.5 = bf16[8,1,64,128]{3,2,1,0:T(8,128)(2,1)S(1)} all-to-all(bf16[8,1,64,128]{3,2,1,0:T(8,128)(2,1)S(1)} %copy.12), channel_id=1, replica_groups=mesh['gx'=8,'gy_0'=2,'gy_1'=8,'gz'=8] {'gz'}, dimensions={0} | all-to-all | bytes 262144 | tf_op jit(solution)/shard_map/all_to_all | solution.py:53
  137.1 0.2 copy.13
  137.3 0.1 copy.14
  137.4 0.8 copy.15
  (1 shorter events, 0.0 us)
Async XLA Ops:
  6.5 1.3 copy-start
  6.5 78.4 %reduce-scatter.3.cloned.1.call-start = ((), (), s32[]{:S(2)}) async-start(), calls=%async_computation.3 | async-start | bytes 4718592 | tf_op jit(solution)/shard_map/reduce_scatter | solution.py:15
  10.9 108.9 %reduce-scatter.5.cloned.1.call-start = ((), (), s32[]{:S(2)}) async-start(), calls=%async_computation.4 | async-start | bytes 786432 | tf_op jit(solution)/shard_map/reduce_scatter | solution.py:15
Sparse Core Ops, SparseCore 0:
  11.0 73.9 reduce-scatter.2
  88.3 31.3 reduce-scatter.4
where the time goes:
time: 145 us
  waiting for transfers between devices  108 us (74%)
  blocking collectives  15.9 us (11%)
  between operations  14.1 us (10%)
  local copies, waits for them, and re-layouts  6.04 us (4%)
    reduce_scatter x2, waiting for transfers between devices, sum_in_order(): parts = lax.psum_scatter(parts, axes[k], scatter_dimension=0, tiled=True)  108 us
    all_to_all x1, blocking collectives, local(): lax.all_to_all(parts, 'gz', split_axis=0, concat_axis=0, tiled=True)  15.9 us
  transfers between devices with their start and end apart: 2, of which 2 were waited for; matrix products, arithmetic and copies ran while one was open for 0% of the time, Pallas kernels for 0%

commit v1 on v0

v1 whole, which is shorter than its diff:
```python
import jax
import jax.numpy as jnp
from jax import lax
from jax.experimental import pallas as pl
from jax.experimental.pallas import tpu as pltpu
from jax.sharding import Mesh
from jax.sharding import PartitionSpec as P

MESH = pl.DeviceIdType.MESH
RING = 8
BF16 = jnp.bfloat16
F32 = jnp.float32


def project(
    e_ref, len_ref, w_ref, out_ref,
    states, staged, weights, acc, perm, parts, arrived,
    far_send, far_recv, y_send, y_recv, z_send, z_recv, chip_send, chip_recv,
):
    xh, z, y, c = (lax.axis_index(a) for a in ("xh", "z", "y", "c"))
    other = 1 - xh
    mate = {"xh": other}
    twin = {"c": 1 - c}
    upper, quarter = y // 4, lax.rem(y, 4)

    def turn(base, by):
        return lax.rem(base + by + 2 * RING, RING)

    def remote(src, dst, send, recv, to):
        return pltpu.make_async_remote_copy(
            src_ref=src, dst_ref=dst, send_sem=send, recv_sem=recv, device_id=to, device_id_type=MESH
        )

    barrier = pltpu.get_barrier_semaphore()

    def greet(i, carry):
        pl.semaphore_signal(barrier, inc=1, device_id={"z": turn(z, i)}, device_id_type=MESH)
        pl.semaphore_signal(barrier, inc=1, device_id={"y": turn(y, i)}, device_id_type=MESH)
        return carry

    lax.fori_loop(1, RING, greet, 0)
    pl.semaphore_signal(barrier, inc=1, device_id=mate, device_id_type=MESH)
    pl.semaphore_signal(barrier, inc=1, device_id=twin, device_id_type=MESH)
    pl.semaphore_wait(barrier, 2 * (RING - 1) + 2)

    e_far = remote(e_ref.at[upper, :, quarter], staged, far_send.at[0], far_recv.at[0], mate)
    e_far.start()
    w_far = remote(
        w_ref.at[pl.ds(c * 128, 128), pl.ds(pl.multiple_of(other * 512, 512), 512)],
        weights.at[z, xh, c], far_send.at[1], far_recv.at[1], mate,
    )
    w_far.start()
    w_far_in = remote(
        weights.at[z, other, c], weights.at[z, other, c], far_send.at[1], far_recv.at[1], mate
    )

    def spread(i, carry):
        to = turn(z, i)
        remote(
            e_ref.at[upper, to, quarter], states.at[y, xh, z], far_send.at[2], far_recv.at[2], {"z": to}
        ).start()
        return carry

    def spread_far(i, carry):
        to = turn(z, i)
        remote(
            staged.at[to], states.at[y, other, z], far_send.at[3], far_recv.at[3], {"z": to}
        ).start()
        return carry

    def seven(block, k):
        some = states.at[y, block, pl.ds(0, RING - 1)]
        return remote(some, some, far_send.at[k], far_recv.at[k], {"z": z})

    lax.fori_loop(1, RING, spread, 0)

    way = 1 - 2 * c
    ahead = {"z": turn(z, way)}

    def w_slot(phase, hop, short):
        source = turn(z, -way * hop)
        half = 1 - c if short else c
        return weights.at[source, xh if phase == 0 else other, half]

    def w_index(phase, hop, short):
        return phase * 7 + (hop - 1) * 2 + short

    def w_send(phase, hop, short, src):
        k = w_index(phase, hop + 1, short)
        remote(src, w_slot(phase, hop, short), z_send.at[k], z_recv.at[k], ahead).start()

    def w_take(phase, hop, short):
        k = w_index(phase, hop, short)
        slot = w_slot(phase, hop, short)
        remote(slot, slot, z_send.at[k], z_recv.at[k], ahead).wait_recv()
        if hop < 3 or (hop == 3 and not short):
            w_send(phase, hop, short, slot)
        remote(slot, slot, chip_send.at[k], chip_recv.at[k], twin).start()

    def own_weight(half):
        return w_ref.at[pl.ds(half * 128, 128), pl.ds(pl.multiple_of(xh * 512, 512), 512)]

    for short in (0, 1):
        w_send(0, 0, short, own_weight(1 - c if short else c))

    def y_slot(block, side, hop):
        source = turn(y, -hop if side == 0 else hop)
        return states.at[source, xh if block == 0 else other]

    def y_index(block, side, hop):
        return (block * 2 + side) * 4 + hop - 1

    def y_send_on(block, side, hop):
        k = y_index(block, side, hop + 1)
        slot = y_slot(block, side, hop)
        to = {"y": turn(y, 1 if side == 0 else -1)}
        remote(slot, slot, y_send.at[k], y_recv.at[k], to).start()

    def y_hops(block, side):
        return 4 if block == side else 3

    def y_take(block, side, hop):
        k = y_index(block, side, hop)
        slot = y_slot(block, side, hop)
        to = {"y": turn(y, 1 if side == 0 else -1)}
        remote(slot, slot, y_send.at[k], y_recv.at[k], to).wait_recv()
        if hop < y_hops(block, side):
            y_send_on(block, side, hop)

    states[y, xh, z] = e_ref[upper, z, quarter]
    for half in (0, 1):
        weights[z, xh, half] = w_ref[pl.ds(half * 128, 128), pl.ds(pl.multiple_of(xh * 512, 512), 512)]
    acc[...] = jnp.zeros_like(acc)

    def build(i, carry):
        column = lax.broadcasted_iota(jnp.int32, (1, 1024), 1)
        lane = lax.rem(column, 128)
        wanted = (
            (lane // 64) * 512
            + (lax.rem(lane, 64) // 16) * 128
            + (lax.rem(lane, 16) // 8) * 64
            + (column // 128) * 8
            + lax.rem(lane, 8)
        )
        row = lax.broadcasted_iota(jnp.int32, (64, 1024), 0) + i * 64
        perm[pl.ds(pl.multiple_of(i * 64, 64), 64), :] = jnp.where(row == wanted, 1.0, 0.0).astype(BF16)
        return carry

    lax.fori_loop(0, 16, build, 0)

    def multiply(block):
        side = xh if block == 0 else other

        def step(i, carry):
            left = states[:, side, i].reshape(128, 256)
            right = weights[i, side].reshape(256, 512)
            acc[...] += jnp.dot(left, right, preferred_element_type=F32)
            return carry

        lax.fori_loop(0, RING, step, 0)

    def chip_wait(phase):
        for k in range(phase * 7, phase * 7 + 7):
            hop, short = (k - phase * 7) // 2 + 1, (k - phase * 7) % 2
            source = turn(z, way * hop)
            half = c if short else 1 - c
            slot = weights.at[source, xh if phase == 0 else other, half]
            remote(slot, slot, chip_send.at[k], chip_recv.at[k], twin).wait_recv()

    seven(xh, 2).wait_recv()
    for side in (0, 1):
        y_send_on(0, side, 0)
    w_take(0, 1, 0)
    w_take(0, 1, 1)
    e_far.wait_recv()
    lax.fori_loop(1, RING, spread_far, 0)
    states[y, other, z] = staged[z]
    w_take(0, 2, 0)
    for side in (0, 1):
        y_take(0, side, 1)
    w_take(0, 2, 1)
    w_take(0, 3, 0)
    for side in (0, 1):
        y_take(0, side, 2)
    w_take(0, 3, 1)
    w_far_in.wait_recv()
    remote(
        weights.at[z, other, c], weights.at[z, other, c], chip_send.at[14], chip_recv.at[14], twin
    ).start()
    w_send(1, 0, 0, weights.at[z, other, c])
    seven(other, 3).wait_recv()
    for side in (0, 1):
        y_send_on(1, side, 0)
    theirs = weights.at[z, other, 1 - c]
    remote(theirs, theirs, chip_send.at[14], chip_recv.at[14], twin).wait_recv()
    w_send(1, 0, 1, theirs)
    w_take(0, 4, 0)
    for side in (0, 1):
        y_take(0, side, 3)
    for side in (0, 1):
        y_take(1, side, 1)
    w_take(1, 1, 0)
    w_take(1, 1, 1)
    y_take(0, 0, 4)
    for side in (0, 1):
        y_take(1, side, 2)
    w_take(1, 2, 0)
    w_take(1, 2, 1)
    chip_wait(0)
    multiply(0)
    for side in (0, 1):
        y_take(1, side, 3)
    w_take(1, 3, 0)
    w_take(1, 3, 1)
    y_take(1, 1, 4)
    w_take(1, 4, 0)
    chip_wait(1)
    multiply(1)

    row = lax.broadcasted_iota(jnp.int32, (128, 512), 0)
    place = (row // 64) * 512 + z * 64 + lax.rem(row, 64)
    total = acc[...]
    kept = jnp.where(place < len_ref[0], total, jnp.zeros_like(total)).astype(BF16).reshape(2, 2, 32, 512)
    sorted_parts = jnp.dot(
        kept[:, 0].reshape(64, 512), perm[pl.ds(0, 512), :], preferred_element_type=F32
    ) + jnp.dot(kept[:, 1].reshape(64, 512), perm[pl.ds(512, 512), :], preferred_element_type=F32)
    sorted_parts = sorted_parts.astype(BF16)
    for b in (0, 1):
        for j in range(RING):
            parts[b * RING + j] = sorted_parts[b * 32 : b * 32 + 32, j * 128 : j * 128 + 128]

    e_far.wait_send()
    w_far.wait_send()
    seven(xh, 2).wait_send()
    seven(other, 3).wait_send()
    for phase in (0, 1):
        for k in range(7):
            slot = w_slot(phase, k // 2 + 1, k % 2)
            k = phase * 7 + k
            remote(slot, slot, z_send.at[k], z_recv.at[k], ahead).wait_send()
            remote(slot, slot, chip_send.at[k], chip_recv.at[k], twin).wait_send()
    remote(theirs, theirs, chip_send.at[14], chip_recv.at[14], twin).wait_send()
    for block in (0, 1):
        for side in (0, 1):
            for hop in range(1, y_hops(block, side) + 1):
                k = y_index(block, side, hop)
                slot = y_slot(block, side, hop)
                remote(slot, slot, y_send.at[k], y_recv.at[k], {"y": y}).wait_send()

    me = xh * RING + y

    def deliver(i, carry):
        to = lax.rem(me + i, 2 * RING)
        remote(
            parts.at[to], arrived.at[me], far_send.at[4], far_recv.at[4],
            {"xh": to // RING, "y": lax.rem(to, RING)},
        ).start()
        return carry

    lax.fori_loop(1, 2 * RING, deliver, 0)
    arrived[me] = parts[me]
    most = arrived.at[pl.ds(0, 2 * RING - 1)]
    last = remote(most, most, far_send.at[4], far_recv.at[4], mate)
    last.wait_recv()
    out_ref[...] = arrived[...]
    last.wait_send()


def local(encoded, lengths, kv_weight):
    states = encoded.reshape(2, 8, 4, 16, 256)
    weight = kv_weight.reshape(256, 1024)
    vmem = pl.BlockSpec(memory_space=pltpu.VMEM)
    arrived = pl.pallas_call(
        project,
        out_shape=jax.ShapeDtypeStruct((16, 32, 128), BF16),
        in_specs=[vmem, pl.BlockSpec(memory_space=pltpu.SMEM), vmem],
        out_specs=vmem,
        scratch_shapes=[
            pltpu.VMEM((8, 2, 8, 16, 256), BF16),
            pltpu.VMEM((8, 16, 256), BF16),
            pltpu.VMEM((8, 2, 2, 128, 512), BF16),
            pltpu.VMEM((128, 512), F32),
            pltpu.VMEM((1024, 1024), BF16),
            pltpu.VMEM((16, 32, 128), BF16),
            pltpu.VMEM((16, 32, 128), BF16),
            pltpu.SemaphoreType.DMA((5,)),
            pltpu.SemaphoreType.DMA((5,)),
            pltpu.SemaphoreType.DMA((16,)),
            pltpu.SemaphoreType.DMA((16,)),
            pltpu.SemaphoreType.DMA((14,)),
            pltpu.SemaphoreType.DMA((14,)),
            pltpu.SemaphoreType.DMA((15,)),
            pltpu.SemaphoreType.DMA((15,)),
        ],
        compiler_params=pltpu.CompilerParams(collective_id=0, has_side_effects=True),
        name="project",
    )(states, lengths, weight)
    arrived = arrived.reshape(2, 8, 32, 2, 4, 2, 8)
    return jnp.transpose(arrived, (3, 2, 6, 5, 1, 0, 4)).reshape(1, 64, 8, 128)


def solution(mesh):
    torus = Mesh(mesh.devices.reshape(4, 2, 2, 8, 8), ("xl", "c", "xh", "z", "y"))
    placed = (P(("xl", "c"), None, ("xh", "z")), P(("xl", "c")), P(("xh", "z"), "y", None))
    return jax.shard_map(
        local, mesh=torus, in_specs=placed, out_specs=P(("xl", "c"), ("xh", "z"), "y", None), check_vma=False
    )
```

time: 145 us -> 73.4 us (0.51)
  the two profiles are of different devices: /device:TPU:2 before, /device:TPU:1 now
where the time goes in v1:
time: 73.4 us; the launch traced here: 73.2 us
  Pallas kernels  67.8 us (92%)
  local copies, waits for them, and re-layouts  4.71 us (6%)
    pallas_call x1, Pallas kernels, local(): pl.pallas_call(project, out_shape=jax.ShapeDtypeStruct((16, 32, 128), BF1...  67.8 us
    unnamed x1, local copies, waits for them, and re-layouts  1.93 us

profile of v1, /device:TPU:1, one launch (start us, length us, event | category | flops | bytes accessed | tf_op | source)
XLA Modules:
  0.0 73.2 jit_solution(17210131187890835108)
XLA Ops:
  0.7 1.9 %copy.10 = bf16[32,8,8,128]{3,1,2,0:T(8,128)(2,1)} copy(bf16[32,8,8,128]{3,2,1,0:T(8,128)(2,1)} %bitcast.12) | data formatting | bytes 1048576
  2.6 67.8 %project.1 = bf16[16,32,128]{2,1,0:T(8,128)(2,1)} custom-call(bf16[2,8,4,16,256]{4,3,2,1,0:T(8,128)(2,1)} %bitcast.13, s32[1]{0:T(128)S(6)} %copy.11.len_ref, bf16[256,1024]{1,0:T(8,128)(2,1)} %bitcast.11), custom_call_target="tpu_custom_call" | custom-call | tf_op jit(solution)/shard_map/project/pallas_call | solution.py:273
  70.4 1.2 %copy.5 = bf16[16,32,128]{1,2,0:T(8,128)(2,1)S(1)} copy(bf16[16,32,128]{2,1,0:T(8,128)(2,1)} %project.1) | data formatting | bytes 262144 | tf_op jit(solution)/shard_map/project/pallas_call | solution.py:273
  71.6 0.5 copy.6
  72.1 0.2 reshape.15
  72.4 0.8 %copy.7 = bf16[1,64,8,128]{3,2,1,0:T(8,128)(2,1)} copy(bf16[1,64,8,128]{1,3,2,0:T(8,128)(2,1)S(1)} %reshape.15) | data formatting | bytes 262144 | tf_op jit(solution)/shard_map/reshape | solution.py:299

commit v2 on v0

v2 whole, which is shorter than its diff:
```python
import jax
import jax.numpy as jnp
from jax import lax
from jax.experimental import pallas as pl
from jax.experimental.pallas import tpu as pltpu
from jax.sharding import Mesh
from jax.sharding import PartitionSpec as P

MESH = pl.DeviceIdType.MESH
RING = 8
BF16 = jnp.bfloat16
F32 = jnp.float32


def project(
    e_in, len_ref, w_in, out_ref,
    e_ref, w_raw, w_ref, states, staged, weights, acc, perm, final, parts, arrived,
    load, far_send, far_recv, e_send, e_recv, y_send, y_recv, z_send, z_recv, chip_send, chip_recv,
):
    xh, z, y, c = (lax.axis_index(a) for a in ("xh", "z", "y", "c"))
    other = 1 - xh
    mate = {"xh": other}
    twin = {"c": 1 - c}
    upper, quarter = y // 4, lax.rem(y, 4)

    def turn(base, by):
        return lax.rem(base + by + 2 * RING, RING)

    def remote(src, dst, send, recv, to):
        return pltpu.make_async_remote_copy(
            src_ref=src, dst_ref=dst, send_sem=send, recv_sem=recv, device_id=to, device_id_type=MESH
        )

    def signal(sem, to):
        pl.semaphore_signal(sem, inc=1, device_id=to, device_id_type=MESH)

    barrier = pltpu.get_barrier_semaphore()

    def greet(i, carry):
        signal(barrier, {"z": turn(z, i)})
        return carry

    lax.fori_loop(1, RING, greet, 0)
    for dy in (1, -1, 2, -2):
        signal(barrier, {"y": turn(y, dy)})
    signal(barrier, mate)
    signal(barrier, twin)
    w_load = pltpu.make_async_copy(w_in, w_raw, load.at[0])
    w_load.start()
    e_load = pltpu.make_async_copy(e_in, e_ref, load.at[1])
    e_load.start()
    w_load.wait()
    for e in range(8):
        w_ref[:, e * 128 : e * 128 + 128] = w_raw[:, e, :]
    e_load.wait()
    pl.semaphore_wait(barrier, RING - 1 + 6)

    def far_weights(sub):
        return remote(
            w_ref.at[pl.ds(c * 128 + sub * 64, 64), pl.ds(pl.multiple_of(other * 512, 512), 512)],
            weights.at[z, xh, c * 2 + sub], far_send.at[1 + sub], far_recv.at[1 + sub], mate,
        )

    w_far = [far_weights(sub) for sub in (0, 1)]
    for sub in (0, 1):
        w_far[sub].start()
    e_far = remote(e_ref.at[upper, :, quarter], staged, far_send.at[0], far_recv.at[0], mate)
    e_far.start()

    way = 1 - 2 * c
    next_z = turn(z, way)
    ahead = {"z": next_z}

    def w_slot(phase, hop, short, sub):
        source = turn(z, -way * hop)
        half = 1 - c if short else c
        return weights.at[source, xh if phase == 0 else other, half * 2 + sub]

    def w_index(phase, hop, short, sub):
        return phase * 14 + (hop - 1) * 4 + short * 2 + sub

    def w_send(phase, hop, short, sub, src):
        k = w_index(phase, hop + 1, short, sub)
        remote(src, w_slot(phase, hop, short, sub), z_send.at[k], z_recv.at[k], ahead).start()

    def w_take(phase, hop, short):
        for sub in (0, 1):
            k = w_index(phase, hop, short, sub)
            slot = w_slot(phase, hop, short, sub)
            remote(slot, slot, z_send.at[k], z_recv.at[k], ahead).wait_recv()
            if hop < 3 or (hop == 3 and not short):
                w_send(phase, hop, short, sub, slot)
            remote(slot, slot, chip_send.at[k], chip_recv.at[k], twin).start()

    def own_weight(short):
        half = 1 - c if short else c
        for sub in (0, 1):
            w_send(
                0, 0, short, sub,
                w_ref.at[pl.ds(half * 128 + sub * 64, 64), pl.ds(pl.multiple_of(xh * 512, 512), 512)],
            )

    def far_own():
        for sub in (0, 1):
            slot = weights.at[z, other, c * 2 + sub]
            remote(slot, slot, far_send.at[1 + sub], far_recv.at[1 + sub], mate).wait_recv()
            w_send(1, 0, 0, sub, slot)
            remote(slot, slot, chip_send.at[28 + sub], chip_recv.at[28 + sub], twin).start()

    def twin_own():
        for sub in (0, 1):
            slot = weights.at[z, other, (1 - c) * 2 + sub]
            remote(slot, slot, chip_send.at[28 + sub], chip_recv.at[28 + sub], twin).wait_recv()
            w_send(1, 0, 1, sub, slot)

    own_weight(0)

    def spread(to, carry):
        @pl.when(to != z)
        def _():
            remote(
                e_ref.at[upper, to, quarter], states.at[y, xh, z], e_send.at[to], e_recv.at[z], {"z": to}
            ).start()

        return carry

    def spread_far(to, carry):
        @pl.when(to != z)
        def _():
            remote(
                staged.at[to], states.at[y, other, z], e_send.at[RING + to], e_recv.at[RING + z], {"z": to}
            ).start()

        return carry

    def take_states(block, first, end):
        def one(source, carry):
            @pl.when(source != z)
            def _():
                slot = states.at[y, xh if block == 0 else other, source]
                k = block * RING + source
                remote(slot, slot, e_send.at[k], e_recv.at[k], {"z": z}).wait_recv()

            return carry

        lax.fori_loop(first, end, one, 0)

    lax.fori_loop(0, RING, spread, 0)
    own_weight(1)

    def far_states():
        e_far.wait_recv()
        lax.fori_loop(0, RING, spread_far, 0)
        states[y, other, z] = staged[z]

    REACH = ((4, 3), (3, 4))

    def y_index(block, side, distance):
        return (block * 2 + side) * 4 + distance - 1

    def y_copy(block, side, origin, distance):
        sign = 1 if side == 0 else -1
        slot = states.at[turn(y, -sign * origin), xh if block == 0 else other]
        k = y_index(block, side, distance)
        return remote(slot, slot, y_send.at[k], y_recv.at[k], {"y": turn(y, sign * (distance - origin))})

    def y_own(block):
        for distance in (2, 1):
            for side in (0, 1):
                y_copy(block, side, 0, distance).start()

    def y_relay(block):
        for side in (block, 1 - block):
            y_copy(block, side, 2, 2).wait_recv()
            for distance in range(REACH[block][side], 2, -1):
                y_copy(block, side, 2, distance).start()

    def y_rest(block):
        for distance in (1, 3, 4):
            for side in (0, 1):
                if distance <= REACH[block][side]:
                    y_copy(block, side, distance, distance).wait_recv()

    states[y, xh, z] = e_ref[upper, z, quarter]
    for q in range(4):
        weights[z, xh, q] = w_ref[q * 64 : q * 64 + 64, pl.ds(pl.multiple_of(xh * 512, 512), 512)]
    acc[...] = jnp.zeros_like(acc)

    column = lax.broadcasted_iota(jnp.int32, (1, 1024), 1)
    lane = lax.rem(column, 128)
    by_owner = (
        (lane // 64) * 512
        + (lax.rem(lane, 64) // 16) * 128
        + (lax.rem(lane, 16) // 8) * 64
        + (column // 128) * 8
        + lax.rem(lane, 8)
    )
    by_head = (
        (lax.rem(lane, 64) // 8) * 128
        + (lax.rem(lane, 8) // 4) * 64
        + lax.rem(lane, 4) * 16
        + (lane // 64) * 8
        + column // 128
    )

    def build(i, carry):
        row = lax.broadcasted_iota(jnp.int32, (64, 1024), 0) + i * 64
        here = pl.ds(pl.multiple_of(i * 64, 64), 64)
        perm[here, :] = jnp.where(row == by_owner, 1.0, 0.0).astype(BF16)
        final[here, :] = jnp.where(row == by_head, 1.0, 0.0).astype(BF16)
        return carry

    lax.fori_loop(0, 16, build, 0)

    def multiply(block, distances):
        side = xh if block == 0 else other
        total = acc[...]
        for d in distances:
            i = turn(z, d)
            total = total + jnp.dot(
                states[:, side, i].reshape(128, 256), weights[i, side].reshape(256, 512),
                preferred_element_type=F32,
            )
        acc[...] = total

    def chip_take(phase, hops):
        for hop in hops:
            for short in (0, 1):
                for sub in (0, 1):
                    if hop < 4 or not short:
                        k = w_index(phase, hop, short, sub)
                        half = c if short else 1 - c
                        slot = weights.at[turn(z, way * hop), xh if phase == 0 else other, half * 2 + sub]
                        remote(slot, slot, chip_send.at[k], chip_recv.at[k], twin).wait_recv()

    w_take(0, 1, 0)
    w_take(0, 1, 1)
    take_states(0, 0, RING)
    y_own(0)
    w_take(0, 2, 0)
    w_take(0, 2, 1)
    far_own()
    w_take(0, 3, 0)
    twin_own()
    w_take(0, 3, 1)
    y_relay(0)
    far_states()
    w_take(0, 4, 0)
    w_take(1, 1, 0)
    take_states(1, 0, RING)
    y_own(1)
    w_take(1, 1, 1)
    w_take(1, 2, 0)
    w_take(1, 2, 1)
    w_take(1, 3, 0)
    y_relay(1)
    w_take(1, 3, 1)
    chip_take(0, (1, 2, 3, 4))
    y_rest(0)
    multiply(0, range(8))
    w_take(1, 4, 0)
    y_rest(1)
    chip_take(1, (1, 2))
    multiply(1, (0, 1, 2, 6, 7))
    chip_take(1, (3, 4))
    multiply(1, (3, 4, 5))

    row = lax.broadcasted_iota(jnp.int32, (128, 512), 0)
    place = (row // 64) * 512 + z * 64 + lax.rem(row, 64)
    total = acc[...]
    kept = jnp.where(place < len_ref[0], total, jnp.zeros_like(total)).astype(BF16).reshape(2, 2, 32, 512)
    sorted_parts = jnp.dot(
        kept[:, 0].reshape(64, 512), perm[pl.ds(0, 512), :], preferred_element_type=F32
    ) + jnp.dot(kept[:, 1].reshape(64, 512), perm[pl.ds(512, 512), :], preferred_element_type=F32)
    sorted_parts = sorted_parts.astype(BF16)
    for b in (0, 1):
        for j in range(RING):
            parts[b * RING + j] = sorted_parts[b * 32 : b * 32 + 32, j * 128 : j * 128 + 128]

    e_far.wait_send()
    for sub in (0, 1):
        w_far[sub].wait_send()

    def sent(to, carry):
        @pl.when(to != z)
        def _():
            for k in (to, RING + to):
                slot = states.at[y, xh, z]
                remote(slot, slot, e_send.at[k], e_recv.at[k], {"z": z}).wait_send()

        return carry

    lax.fori_loop(0, RING, sent, 0)
    for phase in (0, 1):
        for k in range(phase * 14, phase * 14 + 14):
            slot = weights.at[z, xh, 0]
            remote(slot, slot, z_send.at[k], z_recv.at[k], ahead).wait_send()
            remote(slot, slot, chip_send.at[k], chip_recv.at[k], twin).wait_send()
    for k in (28, 29):
        slot = weights.at[z, xh, 0]
        remote(slot, slot, chip_send.at[k], chip_recv.at[k], twin).wait_send()
    for block in (0, 1):
        for side in (0, 1):
            for distance in range(1, REACH[block][side] + 1):
                y_copy(block, side, 0, distance).wait_send()

    me = xh * RING + y

    for across in (1, 0):
        for dy in (4, 3, 5, 2, 6, 1, 7, 0):
            if across or dy:
                to_xh, to_y = (other if across else xh), turn(y, dy)
                remote(
                    parts.at[to_xh * RING + to_y], arrived.at[me], far_send.at[3], far_recv.at[3],
                    {"xh": to_xh, "y": to_y},
                ).start()
    arrived[me] = parts[me]
    most = arrived.at[pl.ds(0, 2 * RING - 1)]
    last = remote(most, most, far_send.at[3], far_recv.at[3], mate)
    last.wait_recv()
    rows = [
        jnp.concatenate(
            [arrived[s * RING + j][:, p * 64 : p * 64 + 64] for j in range(RING) for s in (0, 1)], axis=1
        )
        for p in (0, 1)
    ]
    out_ref[...] = jnp.dot(jnp.concatenate(rows, axis=0), final[...], preferred_element_type=F32).astype(BF16)
    last.wait_send()


def local(encoded, lengths, kv_weight):
    states = encoded.reshape(2, 8, 4, 16, 256)
    vmem = pl.BlockSpec(memory_space=pltpu.VMEM)
    hbm = pl.BlockSpec(memory_space=pltpu.HBM)
    keys_values = pl.pallas_call(
        project,
        out_shape=jax.ShapeDtypeStruct((64, 1024), BF16),
        in_specs=[hbm, pl.BlockSpec(memory_space=pltpu.SMEM), hbm],
        out_specs=vmem,
        scratch_shapes=[
            pltpu.VMEM((2, 8, 4, 16, 256), BF16),
            pltpu.VMEM((256, 8, 128), BF16),
            pltpu.VMEM((256, 1024), BF16),
            pltpu.VMEM((8, 2, 8, 16, 256), BF16),
            pltpu.VMEM((8, 16, 256), BF16),
            pltpu.VMEM((8, 2, 4, 64, 512), BF16),
            pltpu.VMEM((128, 512), F32),
            pltpu.VMEM((1024, 1024), BF16),
            pltpu.VMEM((1024, 1024), BF16),
            pltpu.VMEM((16, 32, 128), BF16),
            pltpu.VMEM((16, 32, 128), BF16),
            pltpu.SemaphoreType.DMA((2,)),
            pltpu.SemaphoreType.DMA((4,)),
            pltpu.SemaphoreType.DMA((4,)),
            pltpu.SemaphoreType.DMA((16,)),
            pltpu.SemaphoreType.DMA((16,)),
            pltpu.SemaphoreType.DMA((16,)),
            pltpu.SemaphoreType.DMA((16,)),
            pltpu.SemaphoreType.DMA((28,)),
            pltpu.SemaphoreType.DMA((28,)),
            pltpu.SemaphoreType.DMA((30,)),
            pltpu.SemaphoreType.DMA((30,)),
        ],
        compiler_params=pltpu.CompilerParams(collective_id=0, has_side_effects=True),
        name="project",
    )(states, lengths, kv_weight)
    return keys_values.reshape(1, 64, 8, 128)


def solution(mesh):
    torus = Mesh(mesh.devices.reshape(4, 2, 2, 8, 8), ("xl", "c", "xh", "z", "y"))
    placed = (P(("xl", "c"), None, ("xh", "z")), P(("xl", "c")), P(("xh", "z"), "y", None))
    return jax.shard_map(
        local, mesh=torus, in_specs=placed, out_specs=P(("xl", "c"), ("xh", "z"), "y", None), check_vma=False
    )
```

time: 145 us -> 66.5 us (0.46)
  the two profiles are of different devices: /device:TPU:2 before, /device:TPU:1 now
where the time goes in v2:
time: 66.5 us; the launch traced here: 65.9 us
  Pallas kernels  63.7 us (96%)
  local copies, waits for them, and re-layouts  1.58 us (2%)
    pallas_call x1, Pallas kernels, local(): pl.pallas_call(project, out_shape=jax.ShapeDtypeStruct((64, 1024), BF16),...  63.7 us
    unnamed x1, local copies, waits for them, and re-layouts  1.58 us

profile of v2, /device:TPU:1, one launch (start us, length us, event | category | flops | bytes accessed | tf_op | source)
XLA Modules:
  0.0 65.9 jit_solution(17448607031195736179)
XLA Ops:
  0.7 63.7 %project.1 = bf16[64,1024]{1,0:T(8,128)(2,1)} custom-call(bf16[2,8,4,16,256]{4,3,2,1,0:T(8,128)(2,1)} %bitcast.5, s32[1]{0:T(128)S(6)} %copy.5.len_ref, bf16[256,8,128]{2,1,0:T(8,128)(2,1)} %w_in.1), custom_call_target="tpu_custom_call" | custom-call | tf_op jit(solution)/shard_map/project/pallas_call | solution.py:335
  64.3 1.6 %copy.4 = bf16[8,8,8,128]{3,2,1,0:T(8,128)(2,1)} copy(bf16[8,8,8,128]{3,1,2,0:T(8,128)(2,1)} %bitcast.4) | data formatting | bytes 262144

commit v3 on v2

--- a/solution.py
+++ b/solution.py
@@ -13,8 +13,8 @@
 
 
 def project(
-    e_in, len_ref, w_in, out_ref,
-    e_ref, w_raw, w_ref, states, staged, weights, acc, perm, final, parts, arrived,
+    e_in, len_in, w_in, out_ref,
+    len_ref, e_ref, w_raw, w_ref, states, weights, acc, perm, final, parts, arrived,
     load, far_send, far_recv, e_send, e_recv, y_send, y_recv, z_send, z_recv, chip_send, chip_recv,
 ):
     xh, z, y, c = (lax.axis_index(a) for a in ("xh", "z", "y", "c"))
@@ -34,6 +34,20 @@
     def signal(sem, to):
         pl.semaphore_signal(sem, inc=1, device_id=to, device_id_type=MESH)
 
+    def rows_of(q):
+        half = c if q < 2 else 1 - c
+        return pl.ds(pl.multiple_of(half * 128 + (q % 2) * 64, 64), 64)
+
+    w_load = [pltpu.make_async_copy(w_in.at[rows_of(q)], w_raw.at[rows_of(q)], load.at[q]) for q in range(4)]
+    e_load = pltpu.make_async_copy(e_in, e_ref, load.at[4])
+    len_load = pltpu.make_async_copy(len_in, len_ref, load.at[5])
+    w_load[0].start()
+    w_load[1].start()
+    e_load.start()
+    w_load[2].start()
+    w_load[3].start()
+    len_load.start()
+
     barrier = pltpu.get_barrier_semaphore()
 
     def greet(i, carry):
@@ -45,14 +59,14 @@
         signal(barrier, {"y": turn(y, dy)})
     signal(barrier, mate)
     signal(barrier, twin)
-    w_load = pltpu.make_async_copy(w_in, w_raw, load.at[0])
-    w_load.start()
-    e_load = pltpu.make_async_copy(e_in, e_ref, load.at[1])
-    e_load.start()
-    w_load.wait()
-    for e in range(8):
-        w_ref[:, e * 128 : e * 128 + 128] = w_raw[:, e, :]
-    e_load.wait()
+
+    def lay_out(q):
+        w_load[q].wait()
+        for e in range(8):
+            w_ref[rows_of(q), e * 128 : e * 128 + 128] = w_raw[rows_of(q), e, :]
+
+    lay_out(0)
+    lay_out(1)
     pl.semaphore_wait(barrier, RING - 1 + 6)
 
     def far_weights(sub):
@@ -62,10 +76,10 @@
         )
 
     w_far = [far_weights(sub) for sub in (0, 1)]
-    for sub in (0, 1):
-        w_far[sub].start()
-    e_far = remote(e_ref.at[upper, :, quarter], staged, far_send.at[0], far_recv.at[0], mate)
-    e_far.start()
+    e_far = remote(states.at[y, xh], states.at[y, xh], far_send.at[0], far_recv.at[0], mate)
+    e_far_in = remote(states.at[y, other], states.at[y, other], far_send.at[0], far_recv.at[0], mate)
+    w_far[0].start()
+    w_far[1].start()
 
     way = 1 - 2 * c
     next_z = turn(z, way)
@@ -100,12 +114,11 @@
                 w_ref.at[pl.ds(half * 128 + sub * 64, 64), pl.ds(pl.multiple_of(xh * 512, 512), 512)],
             )
 
-    def far_own():
-        for sub in (0, 1):
-            slot = weights.at[z, other, c * 2 + sub]
-            remote(slot, slot, far_send.at[1 + sub], far_recv.at[1 + sub], mate).wait_recv()
-            w_send(1, 0, 0, sub, slot)
-            remote(slot, slot, chip_send.at[28 + sub], chip_recv.at[28 + sub], twin).start()
+    def far_own(sub):
+        slot = weights.at[z, other, c * 2 + sub]
+        remote(slot, slot, far_send.at[1 + sub], far_recv.at[1 + sub], mate).wait_recv()
+        w_send(1, 0, 0, sub, slot)
+        remote(slot, slot, chip_send.at[28 + sub], chip_recv.at[28 + sub], twin).start()
 
     def twin_own():
         for sub in (0, 1):
@@ -114,6 +127,7 @@
             w_send(1, 0, 1, sub, slot)
 
     own_weight(0)
+    e_load.wait()
 
     def spread(to, carry):
         @pl.when(to != z)
@@ -124,34 +138,21 @@
 
         return carry
 
-    def spread_far(to, carry):
-        @pl.when(to != z)
-        def _():
-            remote(
-                staged.at[to], states.at[y, other, z], e_send.at[RING + to], e_recv.at[RING + z], {"z": to}
-            ).start()
-
-        return carry
-
-    def take_states(block, first, end):
+    def take_states():
         def one(source, carry):
             @pl.when(source != z)
             def _():
-                slot = states.at[y, xh if block == 0 else other, source]
-                k = block * RING + source
-                remote(slot, slot, e_send.at[k], e_recv.at[k], {"z": z}).wait_recv()
+                slot = states.at[y, xh, source]
+                remote(slot, slot, e_send.at[source], e_recv.at[source], {"z": z}).wait_recv()
 
             return carry
 
-        lax.fori_loop(first, end, one, 0)
+        lax.fori_loop(0, RING, one, 0)
 
     lax.fori_loop(0, RING, spread, 0)
+    lay_out(2)
+    lay_out(3)
     own_weight(1)
-
-    def far_states():
-        e_far.wait_recv()
-        lax.fori_loop(0, RING, spread_far, 0)
-        states[y, other, z] = staged[z]
 
     REACH = ((4, 3), (3, 4))
 
@@ -235,20 +236,21 @@
 
     w_take(0, 1, 0)
     w_take(0, 1, 1)
-    take_states(0, 0, RING)
+    take_states()
+    e_far.start()
     y_own(0)
     w_take(0, 2, 0)
     w_take(0, 2, 1)
-    far_own()
+    far_own(0)
+    far_own(1)
     w_take(0, 3, 0)
     twin_own()
     w_take(0, 3, 1)
     y_relay(0)
-    far_states()
     w_take(0, 4, 0)
+    e_far_in.wait_recv()
+    y_own(1)
     w_take(1, 1, 0)
-    take_states(1, 0, RING)
-    y_own(1)
     w_take(1, 1, 1)
     w_take(1, 2, 0)
     w_take(1, 2, 1)
@@ -262,6 +264,7 @@
     y_rest(1)
     chip_take(1, (1, 2))
     multiply(1, (0, 1, 2, 6, 7))
+    len_load.wait()
     chip_take(1, (3, 4))
     multiply(1, (3, 4, 5))
 
@@ -284,9 +287,8 @@
     def sent(to, carry):
         @pl.when(to != z)
         def _():
-            for k in (to, RING + to):
-                slot = states.at[y, xh, z]
-                remote(slot, slot, e_send.at[k], e_recv.at[k], {"z": z}).wait_send()
+            slot = states.at[y, xh, z]
+            remote(slot, slot, e_send.at[to], e_recv.at[to], {"z": z}).wait_send()
 
         return carry
 
@@ -324,7 +326,7 @@
         )
         for p in (0, 1)
     ]
-    out_ref[...] = jnp.dot(jnp.concatenate(rows, axis=0), final[...], preferred_element_type=F32).astype(BF16)
+    out_ref[...] = jnp.dot(jnp.concatenate(rows, axis=0), final[...], preferred_element_type=F32).reshape(64, 8, 128).astype(BF16)
     last.wait_send()
 
 
@@ -334,26 +336,26 @@
     hbm = pl.BlockSpec(memory_space=pltpu.HBM)
     keys_values = pl.pallas_call(
         project,
-        out_shape=jax.ShapeDtypeStruct((64, 1024), BF16),
-        in_specs=[hbm, pl.BlockSpec(memory_space=pltpu.SMEM), hbm],
+        out_shape=pltpu.VMEM((64, 8, 128), BF16),
+        in_specs=[hbm, hbm, hbm],
         out_specs=vmem,
         scratch_shapes=[
+            pltpu.SMEM((1,), jnp.int32),
             pltpu.VMEM((2, 8, 4, 16, 256), BF16),
             pltpu.VMEM((256, 8, 128), BF16),
             pltpu.VMEM((256, 1024), BF16),
             pltpu.VMEM((8, 2, 8, 16, 256), BF16),
-            pltpu.VMEM((8, 16, 256), BF16),
             pltpu.VMEM((8, 2, 4, 64, 512), BF16),
             pltpu.VMEM((128, 512), F32),
             pltpu.VMEM((1024, 1024), BF16),
             pltpu.VMEM((1024, 1024), BF16),
             pltpu.VMEM((16, 32, 128), BF16),
             pltpu.VMEM((16, 32, 128), BF16),
-            pltpu.SemaphoreType.DMA((2,)),
+            pltpu.SemaphoreType.DMA((6,)),
             pltpu.SemaphoreType.DMA((4,)),
             pltpu.SemaphoreType.DMA((4,)),
-            pltpu.SemaphoreType.DMA((16,)),
-            pltpu.SemaphoreType.DMA((16,)),
+            pltpu.SemaphoreType.DMA((8,)),
+            pltpu.SemaphoreType.DMA((8,)),
             pltpu.SemaphoreType.DMA((16,)),
             pltpu.SemaphoreType.DMA((16,)),
             pltpu.SemaphoreType.DMA((28,)),

time: 66.5 us -> 63.2 us (0.950)
  Pallas kernels: 63.7 us -> 61.5 us
  local copies, waits for them, and re-layouts: 1.58 us -> 0.66 us
    pallas_call x1, Pallas kernels: 63.7 us -> 61.5 us  [local(): pl.pallas_call(project, out_shape=pltpu.VMEM((64, 8, 128), BF16), in_spec...]
    unnamed x1, local copies, waits for them, and re-layouts: 1.58 us -> 0.66 us
where the time goes in v3:
time: 63.2 us; the launch traced here: 62.9 us
  Pallas kernels  61.5 us (97%)
  local copies, waits for them, and re-layouts  0.66 us (1%)
  between operations  0.66 us (1%)
    pallas_call x1, Pallas kernels, local(): pl.pallas_call(project, out_shape=pltpu.VMEM((64, 8, 128), BF16), in_spec...  61.5 us

profile of v3, /device:TPU:1, one launch (start us, length us, event | category | flops | bytes accessed | tf_op | source)
XLA Modules:
  0.0 62.9 jit_solution(15125324517034531710)
XLA Ops:
  0.7 61.5 %project.1 = bf16[64,8,128]{2,1,0:T(8,128)(2,1)S(1)} custom-call(bf16[2,8,4,16,256]{4,3,2,1,0:T(8,128)(2,1)} %bitcast.3, s32[1]{0:T(128)S(6)} %copy.6.len_in, bf16[256,8,128]{2,1,0:T(8,128)(2,1)} %w_in.1), custom_call_target="tpu_custom_call" | custom-call | tf_op jit(solution)/shard_map/project/pallas_call | solution.py:337
  62.2 0.7 %copy.5 = bf16[1,64,8,128]{3,2,1,0:T(8,128)(2,1)} copy(bf16[1,64,8,128]{3,2,1,0:T(8,128)(2,1)S(1)} %bitcast.2) | data formatting | bytes 262144

commit v4 on v3

--- a/solution.py
+++ b/solution.py
@@ -126,7 +126,6 @@
             remote(slot, slot, chip_send.at[28 + sub], chip_recv.at[28 + sub], twin).wait_recv()
             w_send(1, 0, 1, sub, slot)
 
-    own_weight(0)
     e_load.wait()
 
     def spread(to, carry):
@@ -150,6 +149,7 @@
         lax.fori_loop(0, RING, one, 0)
 
     lax.fori_loop(0, RING, spread, 0)
+    own_weight(0)
     lay_out(2)
     lay_out(3)
     own_weight(1)
@@ -245,17 +245,17 @@
     far_own(1)
     w_take(0, 3, 0)
     twin_own()
-    w_take(0, 3, 1)
     y_relay(0)
-    w_take(0, 4, 0)
+    w_take(1, 1, 0)
     e_far_in.wait_recv()
     y_own(1)
-    w_take(1, 1, 0)
     w_take(1, 1, 1)
     w_take(1, 2, 0)
     w_take(1, 2, 1)
     w_take(1, 3, 0)
     y_relay(1)
+    w_take(0, 3, 1)
+    w_take(0, 4, 0)
     w_take(1, 3, 1)
     chip_take(0, (1, 2, 3, 4))
     y_rest(0)
@@ -293,14 +293,6 @@
         return carry
 
     lax.fori_loop(0, RING, sent, 0)
-    for phase in (0, 1):
-        for k in range(phase * 14, phase * 14 + 14):
-            slot = weights.at[z, xh, 0]
-            remote(slot, slot, z_send.at[k], z_recv.at[k], ahead).wait_send()
-            remote(slot, slot, chip_send.at[k], chip_recv.at[k], twin).wait_send()
-    for k in (28, 29):
-        slot = weights.at[z, xh, 0]
-        remote(slot, slot, chip_send.at[k], chip_recv.at[k], twin).wait_send()
     for block in (0, 1):
         for side in (0, 1):
             for distance in range(1, REACH[block][side] + 1):
@@ -317,6 +309,14 @@
                     {"xh": to_xh, "y": to_y},
                 ).start()
     arrived[me] = parts[me]
+    for phase in (0, 1):
+        for k in range(phase * 14, phase * 14 + 14):
+            slot = weights.at[z, xh, 0]
+            remote(slot, slot, z_send.at[k], z_recv.at[k], ahead).wait_send()
+            remote(slot, slot, chip_send.at[k], chip_recv.at[k], twin).wait_send()
+    for k in (28, 29):
+        slot = weights.at[z, xh, 0]
+        remote(slot, slot, chip_send.at[k], chip_recv.at[k], twin).wait_send()
     most = arrived.at[pl.ds(0, 2 * RING - 1)]
     last = remote(most, most, far_send.at[3], far_recv.at[3], mate)
     last.wait_recv()

time: 63.2 us -> 62.5 us (0.989)
  no operation moved by 1% of the time
where the time goes in v4:
time: 62.5 us; the launch traced here: 62.3 us
  Pallas kernels  61 us (98%)
  local copies, waits for them, and re-layouts  0.66 us (1%)
  between operations  0.66 us (1%)
    pallas_call x1, Pallas kernels, local(): pl.pallas_call(project, out_shape=pltpu.VMEM((64, 8, 128), BF16), in_spec...  61 us

profile of v4, /device:TPU:1, one launch (start us, length us, event | category | flops | bytes accessed | tf_op | source)
XLA Modules:
  0.0 62.3 jit_solution(13695421702353870037)
XLA Ops:
  0.7 61.0 %project.1 = bf16[64,8,128]{2,1,0:T(8,128)(2,1)S(1)} custom-call(bf16[2,8,4,16,256]{4,3,2,1,0:T(8,128)(2,1)} %bitcast.3, s32[1]{0:T(128)S(6)} %copy.6.len_in, bf16[256,8,128]{2,1,0:T(8,128)(2,1)} %w_in.1), custom_call_target="tpu_custom_call" | custom-call | tf_op jit(solution)/shard_map/project/pallas_call | solution.py:337
  61.7 0.7 %copy.5 = bf16[1,64,8,128]{3,2,1,0:T(8,128)(2,1)} copy(bf16[1,64,8,128]{3,2,1,0:T(8,128)(2,1)S(1)} %bitcast.2) | data formatting | bytes 262144

commit v5 on v4

--- a/solution.py
+++ b/solution.py
@@ -246,9 +246,9 @@
     w_take(0, 3, 0)
     twin_own()
     y_relay(0)
-    w_take(1, 1, 0)
     e_far_in.wait_recv()
     y_own(1)
+    w_take(1, 1, 0)
     w_take(1, 1, 1)
     w_take(1, 2, 0)
     w_take(1, 2, 1)
@@ -257,10 +257,10 @@
     w_take(0, 3, 1)
     w_take(0, 4, 0)
     w_take(1, 3, 1)
+    w_take(1, 4, 0)
     chip_take(0, (1, 2, 3, 4))
     y_rest(0)
     multiply(0, range(8))
-    w_take(1, 4, 0)
     y_rest(1)
     chip_take(1, (1, 2))
     multiply(1, (0, 1, 2, 6, 7))

time: 62.5 us -> 62.4 us (level)
  no operation moved by 1% of the time
where the time goes in v5:
time: 62.4 us; the launch traced here: 62.3 us
  Pallas kernels  61 us (98%)
  local copies, waits for them, and re-layouts  0.66 us (1%)
  between operations  0.66 us (1%)
    pallas_call x1, Pallas kernels, local(): pl.pallas_call(project, out_shape=pltpu.VMEM((64, 8, 128), BF16), in_spec...  61 us

profile of v5, /device:TPU:1, one launch (start us, length us, event | category | flops | bytes accessed | tf_op | source)
XLA Modules:
  0.0 62.3 jit_solution(5331844096776071119)
XLA Ops:
  0.7 61.0 %project.1 = bf16[64,8,128]{2,1,0:T(8,128)(2,1)S(1)} custom-call(bf16[2,8,4,16,256]{4,3,2,1,0:T(8,128)(2,1)} %bitcast.3, s32[1]{0:T(128)S(6)} %copy.6.len_in, bf16[256,8,128]{2,1,0:T(8,128)(2,1)} %w_in.1), custom_call_target="tpu_custom_call" | custom-call | tf_op jit(solution)/shard_map/project/pallas_call | solution.py:337
  61.6 0.7 %copy.5 = bf16[1,64,8,128]{3,2,1,0:T(8,128)(2,1)} copy(bf16[1,64,8,128]{3,2,1,0:T(8,128)(2,1)S(1)} %bitcast.2) | data formatting | bytes 262144

commit v6 on v5

--- a/solution.py
+++ b/solution.py
@@ -240,8 +240,8 @@
     e_far.start()
     y_own(0)
     w_take(0, 2, 0)
+    far_own(0)
     w_take(0, 2, 1)
-    far_own(0)
     far_own(1)
     w_take(0, 3, 0)
     twin_own()

time: 62.4 us -> 62.4 us (level)
  no operation moved by 1% of the time
where the time goes in v6:
time: 62.4 us; the launch traced here: 62.3 us
  Pallas kernels  61 us (98%)
  local copies, waits for them, and re-layouts  0.66 us (1%)
  between operations  0.66 us (1%)
    pallas_call x1, Pallas kernels, local(): pl.pallas_call(project, out_shape=pltpu.VMEM((64, 8, 128), BF16), in_spec...  61 us

profile of v6, /device:TPU:1, one launch (start us, length us, event | category | flops | bytes accessed | tf_op | source)
XLA Modules:
  0.0 62.3 jit_solution(12748560966338594787)
XLA Ops:
  0.7 61.0 %project.1 = bf16[64,8,128]{2,1,0:T(8,128)(2,1)S(1)} custom-call(bf16[2,8,4,16,256]{4,3,2,1,0:T(8,128)(2,1)} %bitcast.3, s32[1]{0:T(128)S(6)} %copy.6.len_in, bf16[256,8,128]{2,1,0:T(8,128)(2,1)} %w_in.1), custom_call_target="tpu_custom_call" | custom-call | tf_op jit(solution)/shard_map/project/pallas_call | solution.py:337
  61.6 0.7 %copy.5 = bf16[1,64,8,128]{3,2,1,0:T(8,128)(2,1)} copy(bf16[1,64,8,128]{3,2,1,0:T(8,128)(2,1)S(1)} %bitcast.2) | data formatting | bytes 262144
